TPU v7x, 32 devices: a whole 2x2x4 slice. The times are simulated.
32 devices in a mesh: dp: 16 (over z, y, core), tensor: 2 (over x).
Axes of the slice: x: 2, y: 2, z: 4, core: 2. Of those that a mesh axis runs over, the one named last changes fastest.
Arguments:
- step: int32 [1], replicated, may hold values from 0 to 999
- activations: bfloat16 [2, 16384, 8192], P(None, 'dp', 'tensor'), may hold values from -6 to 6
- grad_weight: bfloat16 [2, 8192, 28672], P(None, 'tensor', 'dp'), may hold values from -6 to 6
Outputs:
- preconditioned: float32 [8192, 28672], P('tensor', 'dp')
All inputs are finite; a program needn't handle non-finite values.
Results may differ from a plain program's by a relative error of at most 0.0044.
Values may be sent and summed in bfloat16 or wider, within the bound.
No kernel may reach another device: no remote copies, remote signals or barrier semaphores. Data moves between devices by JAX's collectives and lax.ppermute only.
A program may use at most 192 MiB of HBM per device.

v0:
```python
import jax
import jax.numpy as jnp
from jax import lax
from jax.sharding import PartitionSpec as P

BLOCK = 1024
LAYERS = 2
ITERS = 4


def local(step, activations, grad_weight):
    groups = lax.axis_size("dp")
    layer = step[0] % LAYERS
    damping = 0.05 + 0.1 * step[0].astype(jnp.float32) / 1000.0
    acts = lax.dynamic_index_in_dim(activations, layer, 0, keepdims=False)
    grads = lax.dynamic_index_in_dim(grad_weight, layer, 0, keepdims=False)
    tok_rows = acts.shape[0]
    width = acts.shape[1]
    nblock = width // BLOCK
    share = BLOCK // groups
    blocks = acts.reshape(tok_rows, nblock, BLOCK)
    total_tokens = tok_rows * groups
    first = lax.axis_index("dp") * share
    summed = lax.psum(
        jnp.einsum("tkr,tkc->rkc", blocks, blocks, preferred_element_type=jnp.float32), "dp"
    )
    gram_rows = lax.dynamic_slice_in_dim(summed, first, share, 0)
    row_ids = first + lax.broadcasted_iota(jnp.int32, (share, 1, BLOCK), 0)
    col_ids = lax.broadcasted_iota(jnp.int32, (share, 1, BLOCK), 2)
    identity = (row_ids == col_ids).astype(jnp.float32)
    factor = gram_rows / total_tokens + damping * identity
    block_squares = lax.psum(jnp.sum(factor * factor, axis=(0, 2)), "dp")
    largest = lax.pmax(jnp.max(block_squares), "tensor")
    iterate = jnp.broadcast_to(identity / jnp.sqrt(largest), factor.shape)
    for sweep in range(ITERS):
        whole = lax.all_gather(iterate, "dp", axis=0, tiled=True)
        product = jnp.einsum("rkj,jkc->rkc", factor, whole, precision=lax.Precision.HIGHEST)
        iterate = 2.0 * iterate - jnp.einsum(
            "rkj,jkc->rkc", product, whole, precision=lax.Precision.HIGHEST
        )
    inverse = iterate.astype(jnp.bfloat16)
    stacked = grads.reshape(nblock, BLOCK, grads.shape[1])
    result = jnp.einsum(
        "rkc,kcf->krf",
        lax.all_gather(inverse, "dp", axis=0, tiled=True),
        stacked,
        preferred_element_type=jnp.float32,
    )
    return result.reshape(width, grads.shape[1])


def solution(mesh):
    in_specs = (P(), P(None, "dp", "tensor"), P(None, "tensor", "dp"))
    out_specs = P("tensor", "dp")
    return jax.shard_map(local, mesh=mesh, in_specs=in_specs, out_specs=out_specs, check_vma=False)
```

profile of v0, /device:TPU:0, one launch (start us, length us, event | category | flops | bytes accessed | tf_op | source)
XLA Modules:
  0.0 1019.5 jit_solution(3891566731821359104)
XLA Ops:
  6.5 0.0 all-reduce.2.cloned.1.call-start
  7.2 7.9 constant_dynamic-slice_fusion.1
  15.1 12.0 %copy.23 = bf16[1,1024,4096]{1,2,0:T(8,128)(2,1)} copy(bf16[1,1024,4096]{2,1,0:T(8,128)(2,1)} %constant_dynamic-slice_fusion.1) | data formatting | bytes 16777216
  27.1 17.1 %convolution_bitcast_fusion = f32[1024,4,1024]{2,0,1:T(8,128)} fusion(bf16[1024,4,1024]{0,2,1:T(8,128)(2,1)} %bitcast.51), kind=kOutput, calls=%fused_computation | convolution fusion | flops 8589934592 | bytes 25165824 | tf_op jit(solution)/shard_map/tkr,tkc->rkc/dot_general | solution.py:25
  44.2 0.0 all-reduce.2.cloned.1.call-update
  44.3 0.0 all-gather.14.cloned.1.call-start
  44.3 0.1 fusion.18
  44.4 300.7 %all-reduce.2.cloned.1.call-done = f32[1024,4,1024]{2,0,1:T(8,128)} async-done(((f32[1024,4,1024]{2,0,1:T(8,128)}), f32[1024,4,1024]{2,0,1:T(8,128)}) %all-reduce.2.cloned.1.call-update) | async-done | bytes 16777232 | tf_op jit(solution)/shard_map/psum | solution.py:24
  345.1 1.5 multiply_reduce_fusion
  346.6 31.8 %psum.15 = f32[4]{0:T(128)S(1)} all-reduce(f32[4]{0:T(128)S(1)} %multiply_reduce_fusion), channel_id=1, replica_groups=mesh['dp'=16,'tensor'=2] {'dp'}, use_global_device_ids=true, to_apply=%region_2.3 | all-reduce | flops 4 | bytes 32 | tf_op jit(solution)/shard_map/psum | solution.py:32
  378.4 0.6 reduce_max.9
  379.0 5.5 pmax.7
  385.2 0.8 broadcast_multiply_fusion
  386.0 0.0 all-gather.14.cloned.1.call-update
  386.0 0.3 all-gather.6.cloned.1.call-start
  386.3 47.5 %all-gather.14.cloned.1.call-done = f32[1024,1024]{1,0:T(8,128)} async-done(((f32[64,1024]{1,0:T(8,128)}), f32[1024,1024]{1,0:T(8,128)}) %all-gather.14.cloned.1.call-update) | async-done | bytes 4194320 | tf_op jit(solution)/shard_map/all_gather | solution.py:36
  433.8 11.8 %fusion.4 = f32[64,4,1024]{2,0,1:T(8,128)S(1)} fusion(f32[1024,1024]{1,0:T(8,128)} %all-gather.14.cloned.1.call-done, f32[1024,4,1024]{2,0,1:T(8,128)} %all-reduce.2.cloned.1.call-done, s32[]{:T(128)S(6)} %select_n.18, f32[64,1024]{1,0:T(8,128)S(1)} %fusion.18), kind=kOutput, calls=%fused_computation.5 | convolution fusion | flops 3221749760 | bytes 6553604 | tf_op jit(solution)/shard_map/rkj,jkc->rkc/dot_general | solution.py:37
  445.6 12.8 %fusion.10 = f32[64,4,1024]{2,0,1:T(8,128)} fusion(f32[64,4,1024]{2,0,1:T(8,128)S(1)} %fusion.4, f32[1024,1024]{1,0:T(8,128)} %all-gather.14.cloned.1.call-done, f32[64,1024]{1,0:T(8,128)S(1)} %get-tuple-element.5), kind=kOutput, calls=%fused_computation.7 | convolution fusion | flops 3221487616 | bytes 6553600 | tf_op jit(solution)/shard_map/rkj,jkc->rkc/dot_general | solution.py:38
  458.3 0.0 copy-start.4
  458.3 0.0 all-gather.6.cloned.1.call-update
  458.4 0.0 all-gather.8.cloned.1.call-start
  458.4 125.1 %all-gather.6.cloned.1.call-done = f32[1024,4,1024]{2,0,1:T(8,128)} async-done(((f32[64,4,1024]{2,0,1:T(8,128)}), f32[1024,4,1024]{2,0,1:T(8,128)}) %all-gather.6.cloned.1.call-update) | async-done | bytes 16777232 | tf_op jit(solution)/shard_map/all_gather | solution.py:36
  583.5 0.0 copy-start.1
  583.5 15.3 %convolution_bitcast_fusion.6 = f32[64,4,1024]{2,0,1:T(8,128)S(1)} fusion(f32[1024,4,1024]{2,0,1:T(8,128)} %all-gather.6.cloned.1.call-done, f32[1024,4,1024]{2,0,1:T(8,128)} %all-reduce.2.cloned.1.call-done, s32[]{:T(128)S(6)} %select_n.18, f32[64,1024]{1,0:T(8,128)S(1)} %fusion.18), kind=kOutput, calls=%fused_computation.16 | convolution fusion | flops 3221749760 | bytes 19136516 | tf_op jit(solution)/shard_map/rkj,jkc->rkc/dot_general | solution.py:37
  598.8 0.0 copy-done.4
  598.8 0.0 copy-done.1
  598.8 11.8 %fusion.15 = f32[64,4,1024]{2,0,1:T(8,128)} fusion(f32[1024,4,1024]{2,0,1:T(8,128)S(1)} %copy-done.1, f32[64,4,1024]{2,0,1:T(8,128)S(1)} %convolution_bitcast_fusion.6, f32[64,4,1024]{2,0,1:T(8,128)S(1)} %copy-done.4), kind=kOutput, calls=%fused_computation.15 | convolution fusion | flops 3221749760 | bytes 19922944 | tf_op jit(solution)/shard_map/rkj,jkc->rkc/dot_general | solution.py:38
  610.6 0.0 copy-start.5
  610.6 0.0 all-gather.8.cloned.1.call-update
  610.6 0.0 all-gather.10.cloned.1.call-start
  610.7 124.7 %all-gather.8.cloned.1.call-done = f32[1024,4,1024]{2,0,1:T(8,128)} async-done(((f32[64,4,1024]{2,0,1:T(8,128)}), f32[1024,4,1024]{2,0,1:T(8,128)}) %all-gather.8.cloned.1.call-update) | async-done | bytes 16777232 | tf_op jit(solution)/shard_map/all_gather | solution.py:36
  735.4 0.0 copy-start.2
  735.4 15.0 %convolution_bitcast_fusion.4 = f32[64,4,1024]{2,0,1:T(8,128)S(1)} fusion(f32[1024,4,1024]{2,0,1:T(8,128)} %all-gather.8.cloned.1.call-done, f32[1024,4,1024]{2,0,1:T(8,128)} %all-reduce.2.cloned.1.call-done, s32[]{:T(128)S(6)} %select_n.18, f32[64,1024]{1,0:T(8,128)S(1)} %fusion.18), kind=kOutput, calls=%fused_computation.13 | convolution fusion | flops 3221749760 | bytes 19136516 | tf_op jit(solution)/shard_map/rkj,jkc->rkc/dot_general | solution.py:37
  750.4 0.0 copy-done.5
  750.4 0.0 copy-done.2
  750.4 11.8 %fusion.14 = f32[64,4,1024]{2,0,1:T(8,128)} fusion(f32[1024,4,1024]{2,0,1:T(8,128)S(1)} %copy-done.2, f32[64,4,1024]{2,0,1:T(8,128)S(1)} %convolution_bitcast_fusion.4, f32[64,4,1024]{2,0,1:T(8,128)S(1)} %copy-done.5), kind=kOutput, calls=%fused_computation.12 | convolution fusion | flops 3221749760 | bytes 19922944 | tf_op jit(solution)/shard_map/rkj,jkc->rkc/dot_general | solution.py:38
  762.2 0.0 copy-start.3
  762.2 0.0 all-gather.10.cloned.1.call-update
  762.2 0.0 all-gather.12.cloned.1.call-start
  762.3 124.7 %all-gather.10.cloned.1.call-done = f32[1024,4,1024]{2,0,1:T(8,128)} async-done(((f32[64,4,1024]{2,0,1:T(8,128)}), f32[1024,4,1024]{2,0,1:T(8,128)}) %all-gather.10.cloned.1.call-update) | async-done | bytes 16777232 | tf_op jit(solution)/shard_map/all_gather | solution.py:36
  887.0 0.0 copy-start
  887.0 15.0 %convolution_bitcast_fusion.2 = f32[64,4,1024]{2,0,1:T(8,128)S(1)} fusion(f32[1024,4,1024]{2,0,1:T(8,128)} %all-gather.10.cloned.1.call-done, f32[1024,4,1024]{2,0,1:T(8,128)} %all-reduce.2.cloned.1.call-done, s32[]{:T(128)S(6)} %select_n.18, f32[64,1024]{1,0:T(8,128)S(1)} %fusion.18), kind=kOutput, calls=%fused_computation.10 | convolution fusion | flops 3221749760 | bytes 19136516 | tf_op jit(solution)/shard_map/rkj,jkc->rkc/dot_general | solution.py:37
  902.0 0.0 copy-done.3
  902.0 0.0 copy-done
  902.0 11.6 %fusion.16 = bf16[64,4,1024]{2,0,1:T(8,128)(2,1)} fusion(f32[1024,4,1024]{2,0,1:T(8,128)S(1)} %copy-done, f32[64,4,1024]{2,0,1:T(8,128)S(1)} %convolution_bitcast_fusion.2, f32[64,4,1024]{2,0,1:T(8,128)S(1)} %copy-done.3), kind=kOutput, calls=%fused_computation.17 | convolution fusion | flops 3222011904 | bytes 19398656 | tf_op jit(solution)/shard_map/rkj,jkc->rkc/dot_general | solution.py:38
  913.7 0.0 all-gather.12.cloned.1.call-update
  913.7 13.2 %constant_dynamic-slice_fusion = bf16[1,4096,1792]{2,1,0:T(8,128)(2,1)} fusion(bf16[2,4096,1792]{2,1,0:T(8,128)(2,1)} %param.5, s32[]{:T(128)S(6)} %select_n.17), kind=kLoop, calls=%fused_computation.24 | loop fusion | bytes 29360132 | tf_op jit(solution)/shard_map/jit(dynamic_index_in_dim)/dynamic_slice | solution.py:16
  926.9 59.4 %all-gather.12.cloned.1.call-done = bf16[1024,4,1024]{2,0,1:T(8,128)(2,1)} async-done(((bf16[64,4,1024]{2,0,1:T(8,128)(2,1)}), bf16[1024,4,1024]{2,0,1:T(8,128)(2,1)}) %all-gather.12.cloned.1.call-update) | async-done | bytes 8388624 | tf_op jit(solution)/shard_map/all_gather | solution.py:45
  986.3 25.9 %fusion.19 = f32[4,1024,1792]{2,1,0:T(8,128)} fusion(bf16[1024,4,1024]{2,0,1:T(8,128)(2,1)} %all-gather.12.cloned.1.call-done, bf16[4,1024,1792]{2,1,0:T(8,128)(2,1)} %bitcast.50), kind=kOutput, calls=%fused_computation.27 | convolution fusion | flops 15032385536 | bytes 52428800 | tf_op jit(solution)/shard_map/rkc,kcf->krf/dot_general | solution.py:43
  (1 shorter events, 0.0 us)
Async XLA Ops:
  6.5 338.6 %all-reduce.2.cloned.1.call-start = ((), (), s32[]{:S(2)}) async-start(), calls=%async_computation | async-start | bytes 33554432 | tf_op jit(solution)/shard_map/psum | solution.py:24
  44.3 389.5 %all-gather.14.cloned.1.call-start = ((), (), s32[]{:S(2)}) async-start(), calls=%async_computation.5 | async-start | bytes 4456448 | tf_op jit(solution)/shard_map/all_gather | solution.py:36
  386.0 197.5 %all-gather.6.cloned.1.call-start = ((), (), s32[]{:S(2)}) async-start(), calls=%async_computation.1 | async-start | bytes 17825792 | tf_op jit(solution)/shard_map/all_gather | solution.py:36
  458.3 140.4 %copy-start.4 = (f32[64,4,1024]{2,0,1:T(8,128)S(1)}, f32[64,4,1024]{2,0,1:T(8,128)}, u32[]{:S(2)}) copy-start(f32[64,4,1024]{2,0,1:T(8,128)} %fusion.10) | copy-start | bytes 3145732
  458.4 277.0 %all-gather.8.cloned.1.call-start = ((), (), s32[]{:S(2)}) async-start(), calls=%async_computation.2 | async-start | bytes 17825792 | tf_op jit(solution)/shard_map/all_gather | solution.py:36
  583.5 15.3 %copy-start.1 = (f32[1024,4,1024]{2,0,1:T(8,128)S(1)}, f32[1024,4,1024]{2,0,1:T(8,128)}, u32[]{:S(2)}) copy-start(f32[1024,4,1024]{2,0,1:T(8,128)} %all-gather.6.cloned.1.call-done) | copy-start | bytes 50331652
  610.6 139.8 %copy-start.5 = (f32[64,4,1024]{2,0,1:T(8,128)S(1)}, f32[64,4,1024]{2,0,1:T(8,128)}, u32[]{:S(2)}) copy-start(f32[64,4,1024]{2,0,1:T(8,128)} %fusion.15) | copy-start | bytes 3145732
  610.6 276.4 %all-gather.10.cloned.1.call-start = ((), (), s32[]{:S(2)}) async-start(), calls=%async_computation.3 | async-start | bytes 17825792 | tf_op jit(solution)/shard_map/all_gather | solution.py:36
  735.4 15.0 %copy-start.2 = (f32[1024,4,1024]{2,0,1:T(8,128)S(1)}, f32[1024,4,1024]{2,0,1:T(8,128)}, u32[]{:S(2)}) copy-start(f32[1024,4,1024]{2,0,1:T(8,128)} %all-gather.8.cloned.1.call-done) | copy-start | bytes 50331652
  762.2 139.8 %copy-start.3 = (f32[64,4,1024]{2,0,1:T(8,128)S(1)}, f32[64,4,1024]{2,0,1:T(8,128)}, u32[]{:S(2)}) copy-start(f32[64,4,1024]{2,0,1:T(8,128)} %fusion.14) | copy-start | bytes 3145732
  762.2 224.1 %all-gather.12.cloned.1.call-start = ((), (), s32[]{:S(2)}) async-start(), calls=%async_computation.4 | async-start | bytes 8912896 | tf_op jit(solution)/shard_map/all_gather | solution.py:45
  887.0 15.0 %copy-start = (f32[1024,4,1024]{2,0,1:T(8,128)S(1)}, f32[1024,4,1024]{2,0,1:T(8,128)}, u32[]{:S(2)}) copy-start(f32[1024,4,1024]{2,0,1:T(8,128)} %all-gather.10.cloned.1.call-done) | copy-start | bytes 50331652
Sparse Core Ops, SparseCore 0:
  44.4 300.6 all-reduce.1
  386.1 47.5 all-gather.13
  458.5 124.9 all-gather.5
  610.7 124.6 all-gather.7
  762.3 124.6 all-gather.9
  913.8 72.4 all-gather.11
where the time goes:
time: 1020 us
  waiting for transfers between devices  782 us (77%)
  matrix products  148 us (15%)
  blocking collectives  37.3 us (4%)
  local copies, waits for them, and re-layouts  33.2 us (3%)
  between operations  15.4 us (2%)
    all_gather x4, waiting for transfers between devices, local(): whole = lax.all_gather(iterate, 'dp', axis=0, tiled=True)  422 us
    psum x1, waiting for transfers between devices, local(): lax.psum(jnp.einsum('tkr,tkc->rkc', blocks, blocks, preferred_element_typ...  301 us
    all_gather x1, waiting for transfers between devices, local(): lax.all_gather(inverse, 'dp', axis=0, tiled=True)  59.4 us
    dot_general x4, matrix products, local(): jnp.einsum('rkj,jkc->rkc', factor, whole, precision=lax.Precision.HIGHEST)  57 us
    dot_general x4, matrix products, local(): jnp.einsum('rkj,jkc->rkc', product, whole, precision=lax.Precision.HIGHEST)  48 us
    psum x1, blocking collectives, local(): block_squares = lax.psum(jnp.sum(factor * factor, axis=(0, 2)), 'dp')  31.8 us
    dot_general x1, matrix products, local(): jnp.einsum('rkc,kcf->krf', lax.all_gather(inverse, 'dp', axis=0, tiled=Tr...  25.9 us
  transfers between devices with their start and end apart: 6, of which 6 were waited for; matrix products, arithmetic and copies ran while one was open for 1% of the time, Pallas kernels for 0%

commit v1 on v0

--- a/solution.py
+++ b/solution.py
@@ -33,7 +33,9 @@
     largest = lax.pmax(jnp.max(block_squares), "tensor")
     iterate = jnp.broadcast_to(identity / jnp.sqrt(largest), factor.shape)
     for sweep in range(ITERS):
-        whole = lax.all_gather(iterate, "dp", axis=0, tiled=True)
+        whole = jnp.concatenate(
+            lax.all_to_all(jnp.stack([iterate] * lax.axis_size("dp")), "dp", 0, 0), axis=0
+        )
         product = jnp.einsum("rkj,jkc->rkc", factor, whole, precision=lax.Precision.HIGHEST)
         iterate = 2.0 * iterate - jnp.einsum(
             "rkj,jkc->rkc", product, whole, precision=lax.Precision.HIGHEST

time: 1020 us -> 2100 us (2.06)
  blocking collectives: 37.3 us -> 1510 us
  waiting for transfers between devices: 782 us -> 364 us
  local copies, waits for them, and re-layouts: 33.2 us -> 71.1 us
    all_to_all x0 -> x4, blocking collectives: none -> 1470 us  [local(): lax.all_to_all(jnp.stack([iterate] * lax.axis_size('dp')), 'dp', 0, 0)]
    all_gather x4 -> x0, waiting for transfers between devices: 422 us -> none  [local(): whole = lax.all_gather(iterate, 'dp', axis=0, tiled=True)]
    all_to_all x0 -> x4, local copies, waits for them, and re-layouts: none -> 29.4 us  [local(): lax.all_to_all(jnp.stack([iterate] * lax.axis_size('dp')), 'dp', 0, 0)]
  transfers between devices with their start and end apart: 6 -> 2, of which waited for: 6 -> 2; matrix products, arithmetic and copies ran while one was open for 1% -> 1% of each run, Pallas kernels for 0% -> 0%
where the time goes in v1:
time: 2100 us
  blocking collectives  1510 us (72%)
  waiting for transfers between devices  364 us (17%)
  matrix products  136 us (6%)
  local copies, waits for them, and re-layouts  71.1 us (3%)
    all_to_all x4, blocking collectives, local(): lax.all_to_all(jnp.stack([iterate] * lax.axis_size('dp')), 'dp', 0, 0)  1470 us
    psum x1, waiting for transfers between devices, local(): lax.psum(jnp.einsum('tkr,tkc->rkc', blocks, blocks, preferred_element_typ...  301 us
    all_gather x1, waiting for transfers between devices, local(): lax.all_gather(inverse, 'dp', axis=0, tiled=True)  63 us
    dot_general x4, matrix products, local(): jnp.einsum('rkj,jkc->rkc', factor, whole, precision=lax.Precision.HIGHEST)  48.4 us
    dot_general x4, matrix products, local(): jnp.einsum('rkj,jkc->rkc', product, whole, precision=lax.Precision.HIGHEST)  45.3 us
  transfers between devices with their start and end apart: 2, of which 2 were waited for; matrix products, arithmetic and copies ran while one was open for 1% of the time, Pallas kernels for 0%

profile of v1, /device:TPU:0, one launch (start us, length us, event | category | flops | bytes accessed | tf_op | source)
XLA Modules:
  0.0 2095.0 jit_solution(8938493958303505855)
XLA Ops:
  6.5 0.0 all-reduce.2.cloned.1.call-start
  7.2 7.9 constant_dynamic-slice_fusion.1
  15.1 12.0 copy.45
  27.1 17.1 convolution_bitcast_fusion
  44.2 0.0 all-reduce.2.cloned.1.call-update
  44.2 0.0 all-gather.2.cloned.1.call-start
  44.3 0.1 fusion.6
  44.4 300.7 %all-reduce.2.cloned.1.call-done = f32[1024,4,1024]{2,0,1:T(8,128)} async-done(((f32[1024,4,1024]{2,0,1:T(8,128)}), f32[1024,4,1024]{2,0,1:T(8,128)}) %all-reduce.2.cloned.1.call-update) | async-done | bytes 16777232 | tf_op jit(solution)/shard_map/psum | solution.py:24
  345.0 1.5 multiply_reduce_fusion
  346.5 31.8 %psum.15 = f32[4]{0:T(128)S(1)} all-reduce(f32[4]{0:T(128)S(1)} %multiply_reduce_fusion), channel_id=1, replica_groups=mesh['dp'=16,'tensor'=2] {'dp'}, use_global_device_ids=true, to_apply=%region_2.3 | all-reduce | flops 4 | bytes 32 | tf_op jit(solution)/shard_map/psum | solution.py:32
  378.3 0.6 reduce_max.9
  378.9 5.5 pmax.7
  385.2 0.1 broadcast_multiply_fusion
  385.3 2.1 stack.8
  387.4 365.4 %all_to_all.20 = f32[16,64,4,1024]{3,1,2,0:T(8,128)} all-to-all(f32[16,64,4,1024]{3,1,2,0:T(8,128)S(1)} %stack.8), channel_id=1, replica_groups=mesh['dp'=16,'tensor'=2] {'dp'}, dimensions={0} | all-to-all | bytes 33554432 | tf_op jit(solution)/shard_map/all_to_all | solution.py:37
  752.8 7.3 copy.39
  760.1 12.1 convolution_bitcast_fusion.8
  772.2 11.3 fusion.3
  783.5 2.1 stack.9
  785.7 367.0 %all_to_all.21 = f32[16,64,4,1024]{3,1,2,0:T(8,128)} all-to-all(f32[16,64,4,1024]{3,1,2,0:T(8,128)S(1)} %stack.9), channel_id=1, replica_groups=mesh['dp'=16,'tensor'=2] {'dp'}, dimensions={0} | all-to-all | bytes 33554432 | tf_op jit(solution)/shard_map/all_to_all | solution.py:37
  1152.7 7.3 copy.40
  1159.9 12.1 convolution_bitcast_fusion.6
  1172.0 11.1 fusion.2
  1183.1 2.1 stack.10
  1185.3 368.2 %all_to_all.22 = f32[16,64,4,1024]{3,1,2,0:T(8,128)} all-to-all(f32[16,64,4,1024]{3,1,2,0:T(8,128)S(1)} %stack.10), channel_id=1, replica_groups=mesh['dp'=16,'tensor'=2] {'dp'}, dimensions={0} | all-to-all | bytes 33554432 | tf_op jit(solution)/shard_map/all_to_all | solution.py:37
  1553.4 7.5 copy.41
  1560.9 12.1 convolution_bitcast_fusion.4
  1573.0 11.0 fusion.1
  1584.1 2.1 stack.11
  1586.2 368.2 %all_to_all.23 = f32[16,64,4,1024]{3,1,2,0:T(8,128)} all-to-all(f32[16,64,4,1024]{3,1,2,0:T(8,128)S(1)} %stack.11), channel_id=1, replica_groups=mesh['dp'=16,'tensor'=2] {'dp'}, dimensions={0} | all-to-all | bytes 33554432 | tf_op jit(solution)/shard_map/all_to_all | solution.py:37
  1954.4 7.3 copy.42
  1961.7 12.1 convolution_bitcast_fusion.2
  1973.8 11.9 fusion.4
  1985.7 0.0 all-gather.2.cloned.1.call-update
  1985.7 13.3 constant_dynamic-slice_fusion
  1999.0 63.0 %all-gather.2.cloned.1.call-done = bf16[1024,4,1024]{2,0,1:T(8,128)(2,1)} async-done(((bf16[64,4,1024]{2,0,1:T(8,128)(2,1)}), bf16[1024,4,1024]{2,0,1:T(8,128)(2,1)}) %all-gather.2.cloned.1.call-update) | async-done | bytes 8388624 | tf_op jit(solution)/shard_map/all_gather | solution.py:47
  2062.1 25.7 %fusion.7 = f32[4,1024,1792]{2,1,0:T(8,128)} fusion(bf16[1024,4,1024]{2,0,1:T(8,128)(2,1)} %all-gather.2.cloned.1.call-done, bf16[4,1024,1792]{2,1,0:T(8,128)(2,1)} %bitcast.64), kind=kOutput, calls=%fused_computation.23 | convolution fusion | flops 15032385536 | bytes 52428800 | tf_op jit(solution)/shard_map/rkc,kcf->krf/dot_general | solution.py:45
  (1 shorter events, 0.0 us)
Async XLA Ops:
  6.5 338.5 %all-reduce.2.cloned.1.call-start = ((), (), s32[]{:S(2)}) async-start(), calls=%async_computation.4 | async-start | bytes 33554432 | tf_op jit(solution)/shard_map/psum | solution.py:24
  44.2 2017.8 %all-gather.2.cloned.1.call-start = ((), (), s32[]{:S(2)}) async-start(), calls=%async_computation.5 | async-start | bytes 8912896 | tf_op jit(solution)/shard_map/all_gather | solution.py:47
Sparse Core Ops, SparseCore 0:
  44.3 300.6 all-reduce.1
  1985.9 76.1 all-gather.1
